TPU v7x, 128 devices: a whole 4x4x4 slice. The times are simulated.
128 devices in a mesh: ma: 16 (over x, y), row: 4 (over z_lo, core), col: 2 (over z_hi).
Axes of the slice: x: 4, y: 4, z: 4 (z_hi: 2, z_lo: 2; z = z_hi * 2 + z_lo), core: 2. Of those that a mesh axis runs over, the one named last changes fastest.
Arguments:
- foreground_cols: float32 [131072, 384], P('ma', ('row', 'col')), parts along dimension 0, as said below
- signal_rows: float32 [6144, 8192], P('ma', ('row', 'col')), parts along dimension 0, may hold values from -6 to 6
- visibilities: float32 [131072, 1024], P(('ma', 'row'), 'col'), parts along dimension 0, may hold values from -6 to 6
Outputs:
- factor_cols: float32 [131072, 384], P('ma', ('row', 'col')), parts along dimension 0
- whitened_rows: float32 [6144, 8192], P('ma', ('row', 'col')), parts along dimension 0
- projected: float32 [131072, 1024], P(('ma', 'row'), 'col'), parts along dimension 0
There are 16 independent parts, one for each index of `ma`. A program takes and returns all parts, laid end to end along the dimension named above; each array names one. Nothing has to cross between parts.
Inputs may be any that keep to these rules, and one draw needn't show every extreme that they name: `foreground_cols`: the top 384 rows form a symmetric matrix whose eigenvalues are all 1 or more.
All inputs are finite; a program needn't handle non-finite values.
Results may differ from a plain program's by a relative error of at most 0.0001.
Values sent between devices are 32-bit elements; how exact they have to be, the bound alone decides.
A program may use at most 64 MiB of HBM per device.

v0:
```python
import jax
import jax.numpy as jnp
from jax import lax
from jax.sharding import PartitionSpec as P


def from_everyone(value, axis):
    copies = jnp.broadcast_to(value, (lax.axis_size(axis), *value.shape))
    return lax.all_to_all(copies, axis, split_axis=0, concat_axis=0, tiled=True)


def in_order(pieces, dim):
    lengths = list(pieces.shape[1:])
    lengths[dim] *= pieces.shape[0]
    return jnp.moveaxis(pieces, 0, dim).reshape(lengths)


def collect(value, axis, dim):
    pieces = from_everyone(value, axis)
    return in_order(pieces, dim)


def broadcast(value, axis, root):
    return lax.dynamic_index_in_dim(lax.all_gather(value, axis), root, 0, keepdims=False)


def rows_layout(foreground_cols, signal_rows, visibilities, member, row_index):
    covered = foreground_cols.shape[1] * lax.axis_size(("row", "col"))
    row_block = lax.all_to_all(
        foreground_cols, ("row", "col"), split_axis=0, concat_axis=1, tiled=True
    )
    block_rows = row_block.shape[0]
    top_square = collect(foreground_cols[:covered], ("row", "col"), 1)
    top_factor = jnp.linalg.cholesky(top_square)
    solved = lax.linalg.triangular_solve(
        top_factor, row_block, left_side=False, lower=True, transpose_a=True
    )
    padded_top = jnp.concatenate(
        [top_factor, jnp.zeros((block_rows, covered), jnp.float32)], axis=0
    )
    start = jnp.minimum(member * block_rows, covered)
    top_rows = lax.dynamic_slice_in_dim(padded_top, start, block_rows, 0)
    global_ids = member * block_rows + lax.broadcasted_iota(jnp.int32, solved.shape, 0)
    lower_rows = jnp.where(global_ids < covered, top_rows, solved)
    columns = lax.all_to_all(lower_rows, ("row", "col"), split_axis=1, concat_axis=0, tiled=True)
    whitened = lax.linalg.triangular_solve(top_factor, signal_rows, left_side=True, lower=True)
    own_rows = collect(lower_rows, "col", 0)
    candidate = lax.linalg.triangular_solve(
        top_factor, visibilities[:covered], left_side=True, lower=True
    )
    head_solved = broadcast(candidate, "row", 0)
    remainder = visibilities - jnp.dot(own_rows, head_solved, precision=lax.Precision.HIGHEST)
    placed = lax.dynamic_update_slice_in_dim(remainder, head_solved, 0, 0)
    projected = jnp.where(row_index == 0, placed, remainder)
    return (columns, whitened, projected)


def shards(foreground_cols, signal_rows, visibilities):
    member = lax.axis_index(("row", "col"))
    row_index = lax.axis_index("row")
    return rows_layout(foreground_cols, signal_rows, visibilities, member, row_index)


def solution(mesh):
    return jax.shard_map(
        shards,
        mesh=mesh,
        in_specs=(P("ma", ("row", "col")), P("ma", ("row", "col")), P(("ma", "row"), "col")),
        out_specs=(P("ma", ("row", "col")), P("ma", ("row", "col")), P(("ma", "row"), "col")),
        check_vma=False,
    )
```

profile of v0, /device:TPU:1, one launch (start us, length us, event | category | flops | bytes accessed | tf_op | source)
XLA Modules:
  0.0 249.6 jit_solution(13573841444082139325)
XLA Ops:
  7.2 1.0 slice.114
  9.0 6.8 %all-to-all-start = ((f32[8,384,48]{1,2,0:T(8,128)}), f32[8,384,48]{1,2,0:T(8,128)S(1)}, u32[]{:S(2)}, u32[]{:S(2)}) async-start(f32[8,384,48]{1,2,0:T(8,128)} %broadcast_in_dim.9), calls=%async_computation | async-start | bytes 1179648 | tf_op jit(solution)/shard_map/all_to_all | solution.py:9
  15.8 1.2 copy.54
  17.1 8.8 %all-to-all-done = f32[8,384,48]{1,2,0:T(8,128)S(1)} async-done(((f32[8,384,48]{1,2,0:T(8,128)}), f32[8,384,48]{1,2,0:T(8,128)S(1)}, u32[]{:S(2)}, u32[]{:S(2)}) %all-to-all-start) | async-done | bytes 589856 | tf_op jit(solution)/shard_map/all_to_all | solution.py:9
  25.9 3.8 %all-to-all-start.1 = ((f32[8,1024,48]{1,2,0:T(8,128)}), f32[8,1024,48]{1,2,0:T(8,128)S(1)}, u32[]{:S(2)}, u32[]{:S(2)}) async-start(f32[8,1024,48]{1,2,0:T(8,128)} %bitcast.60), calls=%async_computation.1 | async-start | bytes 3145728 | tf_op jit(solution)/shard_map/all_to_all | solution.py:29
  30.0 11.7 %cholesky.77 = f32[128,128]{1,0:T(8,128)S(1)} custom-call(f32[128,128]{1,0:T(8,128)S(1)} %cholesky.192), custom_call_target="Cholesky" | custom-call | tf_op jit(solution)/shard_map/jit(cholesky)/cholesky | solution.py:34
  41.7 9.8 %custom-call.26 = f32[1,128,128]{1,2,0:T(8,128)S(1)} custom-call(f32[1,128,128]{2,1,0:T(8,128)S(1)} %get-tuple-element.31), custom_call_target="InvertDiagBlocksLowerTriangular" | custom-call | tf_op jit(solution)/shard_map/jit(cholesky)/cholesky | solution.py:34
  52.4 11.7 %cholesky.162 = f32[128,128]{1,0:T(8,128)S(1)} custom-call(f32[128,128]{1,0:T(8,128)S(1)} %cholesky.196), custom_call_target="Cholesky" | custom-call | tf_op jit(solution)/shard_map/jit(cholesky)/cholesky | solution.py:34
  64.2 10.0 %custom-call.27 = f32[1,128,128]{1,2,0:T(8,128)S(1)} custom-call(f32[1,128,128]{2,1,0:T(8,128)S(1)} %get-tuple-element.28), custom_call_target="InvertDiagBlocksLowerTriangular" | custom-call | tf_op jit(solution)/shard_map/jit(cholesky)/cholesky | solution.py:34
  74.6 11.7 %cholesky.181 = f32[128,128]{1,0:T(8,128)S(1)} custom-call(f32[128,128]{1,0:T(8,128)S(1)} %convolution_subtract_fusion.8), custom_call_target="Cholesky" | custom-call | tf_op jit(solution)/shard_map/jit(cholesky)/cholesky | solution.py:34
  90.5 7.9 %while.1 = (s32[]{:T(128)}, f32[384,384]{1,0:T(8,128)S(1)}, s32[3,2]{0,1:T(2,128)S(1)}, f32[3,128,128]{2,1,0:T(8,128)}, s32[]{:T(128)}) while((s32[]{:T(128)}, f32[384,384]{1,0:T(8,128)S(1)}, s32[3,2]{0,1:T(2,128)S(1)}, f32[3,128,128]{2,1,0:T(8,128)}, s32[]{:T(128)}) %tuple.30), condition=%wide.while_cond, body=%wide.while_body.sunk | while | flops 2 | bytes 132705 | solution.py:35
  91.2 2.0 bitcast_dynamic-update-slice_fusion.2
  93.9 2.0 bitcast_dynamic-update-slice_fusion.2
  96.5 2.0 bitcast_dynamic-update-slice_fusion.2
  98.5 30.3 %custom-call.28 = f32[3,128,128]{1,2,0:T(8,128)S(1)} custom-call(f32[3,128,128]{2,1,0:T(8,128)} %get-tuple-element.10), custom_call_target="InvertDiagBlocksLowerTriangular" | custom-call | tf_op jit(solution)/shard_map/triangular_solve | solution.py:35
  128.8 1.4 fusion.18
  130.2 1.3 convolution_subtract_fusion.6
  132.0 1.4 convolution_subtract_fusion.5
  135.7 1.0 copy.49
  137.5 1.2 copy.50
  142.7 41.4 %all_to_all.48 = f32[1024,8,48]{0,2,1:T(8,128)} all-to-all(f32[1024,8,48]{0,2,1:T(8,128)S(1)} %bitcast.71), channel_id=1, replica_groups=mesh['ma'=16,'row'=4,'col'=2] {'row','col'}, dimensions={1} | all-to-all | bytes 3145728 | tf_op jit(solution)/shard_map/all_to_all | solution.py:45
  184.0 1.9 broadcast_in_dim.10
  185.9 4.2 %all-to-all-start.3 = ((f32[2,1024,384]{2,1,0:T(8,128)}), f32[2,1024,384]{2,1,0:T(8,128)S(1)}, u32[]{:S(2)}, u32[]{:S(2)}) async-start(f32[2,1024,384]{2,1,0:T(8,128)} %broadcast_in_dim.10), calls=%async_computation.3 | async-start | bytes 6291456 | tf_op jit(solution)/shard_map/all_to_all | solution.py:9
  190.1 1.7 fusion.16
  191.8 1.7 convolution_subtract_fusion.3
  194.1 1.8 convolution_subtract_fusion.1
  196.6 1.2 pad_maximum_fusion
  198.5 1.2 copy.52
  199.8 27.3 %all-to-all-done.3 = f32[2,1024,384]{2,1,0:T(8,128)S(1)} async-done(((f32[2,1024,384]{2,1,0:T(8,128)}), f32[2,1024,384]{2,1,0:T(8,128)S(1)}, u32[]{:S(2)}, u32[]{:S(2)}) %all-to-all-start.3) | async-done | bytes 3145760 | tf_op jit(solution)/shard_map/all_to_all | solution.py:9
  227.1 12.3 %convolution_subtract_fusion = f32[2048,512]{1,0:T(8,128)S(1)} fusion(f32[2048,512]{1,0:T(8,128)} %param.5, f32[2048,384]{1,0:T(8,128)S(1)} %bitcast.67, f32[1536,512]{1,0:T(8,128)} %all-gather.3.cloned.1.call-done), kind=kOutput, calls=%fused_computation.2 | convolution fusion | flops 4832886784 | bytes 12320768 | tf_op jit(solution)/shard_map/dot_general | solution.py:52
  239.3 1.4 fusion.7
  240.7 2.0 copy-done.1
  (57 shorter events, 16.2 us)
Async XLA Ops:
  7.2 8.7 %copy-start.5 = (f32[8192,48]{0,1:T(8,128)S(1)}, f32[8192,48]{0,1:T(8,128)}, u32[]{:S(2)}) copy-start(f32[8192,48]{0,1:T(8,128)} %param.3) | copy-start | bytes 4718596
  9.0 16.8 %all-to-all-start = ((f32[8,384,48]{1,2,0:T(8,128)}), f32[8,384,48]{1,2,0:T(8,128)S(1)}, u32[]{:S(2)}, u32[]{:S(2)}) async-start(f32[8,384,48]{1,2,0:T(8,128)} %broadcast_in_dim.9), calls=%async_computation | async-start | bytes 1179648 | tf_op jit(solution)/shard_map/all_to_all | solution.py:9
  25.9 108.9 %all-to-all-start.1 = ((f32[8,1024,48]{1,2,0:T(8,128)}), f32[8,1024,48]{1,2,0:T(8,128)S(1)}, u32[]{:S(2)}, u32[]{:S(2)}) async-start(f32[8,1024,48]{1,2,0:T(8,128)} %bitcast.60), calls=%async_computation.1 | async-start | bytes 3145728 | tf_op jit(solution)/shard_map/all_to_all | solution.py:29
  29.7 197.4 %all-gather.3.cloned.1.call-start = ((), (), s32[]{:S(2)}) async-start(), calls=%async_computation.4 | async-start | bytes 3932160 | tf_op jit(solution)/shard_map/all_gather | solution.py:24
  98.5 41.8 %copy-start.2 = (f32[384,384]{1,0:T(8,128)}, f32[384,384]{1,0:T(8,128)S(1)}, u32[]{:S(2)}) copy-start(f32[384,384]{1,0:T(8,128)S(1)} %get-tuple-element.84) | copy-start | bytes 1769476
  137.3 1.5 copy-start.4
  140.3 1.6 copy-start.3
  185.9 41.2 %all-to-all-start.3 = ((f32[2,1024,384]{2,1,0:T(8,128)}), f32[2,1024,384]{2,1,0:T(8,128)S(1)}, u32[]{:S(2)}, u32[]{:S(2)}) async-start(f32[2,1024,384]{2,1,0:T(8,128)} %broadcast_in_dim.10), calls=%async_computation.3 | async-start | bytes 6291456 | tf_op jit(solution)/shard_map/all_to_all | solution.py:9
  196.6 2.0 copy-start
  240.7 2.0 copy-start.1
Sparse Core Ops, SparseCore 0:
  134.9 56.3 all-gather.2
where the time goes:
time: 250 us
  other arithmetic  91.5 us (37%)
  blocking collectives  41.4 us (17%)
  waiting for transfers between devices  36.1 us (14%)
  matrix products  28.5 us (11%)
  local copies, waits for them, and re-layouts  21.1 us (8%)
  between operations  16.3 us (7%)
  starting transfers between devices  14.8 us (6%)
    another operation x10, other arithmetic, rows_layout(): top_factor = jnp.linalg.cholesky(top_square)  56.4 us
    all_to_all x1, blocking collectives, rows_layout(): lax.all_to_all(lower_rows, ('row', 'col'), split_axis=1, concat_axis=0, t...  41.4 us
    all_to_all x2, waiting for transfers between devices, from_everyone(): return lax.all_to_all(copies, axis, split_axis=0, concat_axis=0, tiled=True)  36.1 us
    another operation x3, other arithmetic, rows_layout(): lax.linalg.triangular_solve(top_factor, row_block, left_side=False, lower...  31.2 us
    dot_general x1, matrix products, rows_layout(): jnp.dot(own_rows, head_solved, precision=lax.Precision.HIGHEST)  12.3 us
    all_to_all x2, starting transfers between devices, from_everyone(): return lax.all_to_all(copies, axis, split_axis=0, concat_axis=0, tiled=True)  11 us
    another operation x9, local copies, waits for them, and re-layouts  7.94 us
    another operation x5, matrix products, rows_layout(): lax.linalg.triangular_solve(top_factor, signal_rows, left_side=True, lowe...  6.43 us
  transfers between devices with their start and end apart: 4, of which 2 were waited for; matrix products, arithmetic and copies ran while one was open for 49% of the time, Pallas kernels for 0%

commit v1 on v0

v1 whole, which is shorter than its diff:
```python
import jax
import jax.numpy as jnp
from jax import lax
from jax.experimental import pallas as pl
from jax.experimental.pallas import tpu as pltpu
from jax.sharding import PartitionSpec as P

MESH = pl.DeviceIdType.MESH
F32 = jnp.float32
B = 128
HI = lax.Precision.HIGHEST

def dot(a, b, dims=((1,), (0,))):
    return lax.dot_general(a, b, (dims, ((), ())), precision=HI, preferred_element_type=jnp.float32)

def diag_block(d_ref, e_ref):
    for p in range(B // 8):
        c0 = 8 * p
        rows = pl.ds(c0, 8)
        panel = d_ref[rows, :]
        cols = [jnp.broadcast_to(panel[:, c0 + j:c0 + j + 1], (8, B)) for j in range(8)]
        s = {(i, j): jnp.broadcast_to(cols[j][i:i + 1, :], (8, B)) for j in range(8) for i in range(j, 8)}
        w = [jnp.broadcast_to(panel[i:i + 1, :], (8, B)) for i in range(8)]
        ep = e_ref[rows, :]
        v = [jnp.broadcast_to(ep[i:i + 1, :], (8, B)) for i in range(8)]
        r = []
        for j in range(8):
            r.append(lax.rsqrt(s[j, j]))
            for i in range(j + 1, 8):
                s[i, j] = s[i, j] * r[j]
            for k in range(j + 1, 8):
                for i in range(k, 8):
                    s[i, k] = s[i, k] - s[i, j] * s[k, j]
            w[j] = w[j] * r[j]
            v[j] = v[j] * r[j]
            for i in range(j + 1, 8):
                w[i] = w[i] - s[i, j] * w[j]
                v[i] = v[i] - s[i, j] * v[j]
        for j in range(8):
            d_ref[pl.ds(c0 + j, 1), :] = w[j][:1]
            e_ref[pl.ds(c0 + j, 1), :] = v[j][:1]
        for q in range(p + 1, B // 8):
            rq = pl.ds(8 * q, 8)
            dq = d_ref[rq, :]
            eq = e_ref[rq, :]
            g = [jnp.broadcast_to(dq[:, c0 + j:c0 + j + 1], (8, B)) for j in range(8)]
            for j in range(8):
                g[j] = g[j] * r[j]
                for k in range(j + 1, 8):
                    g[k] = g[k] - g[j] * s[k, j]
                dq = dq - g[j] * w[j]
                eq = eq - g[j] * v[j]
            d_ref[rq, :] = dq
            e_ref[rq, :] = eq

def factor(a_ref, e_ref, d_ref, f_ref):
    n = a_ref.shape[0]
    eye = (lax.broadcasted_iota(jnp.int32, (n, n), 0) == lax.broadcasted_iota(jnp.int32, (n, n), 1))
    e_ref[...] = eye.astype(jnp.float32)
    def step(b, _):
        blk = pl.ds(pl.multiple_of(b * B, B), B)
        d_ref[...] = a_ref[blk, blk]
        f_ref[...] = eye[:B, :B].astype(jnp.float32)
        diag_block(d_ref, f_ref)
        inv = f_ref[...]
        below = lax.broadcasted_iota(jnp.int32, (n, B), 0) >= (b + 1) * B
        left = jnp.where(below, dot(a_ref[:, blk], inv, ((1,), (1,))), 0.0)
        top = dot(inv, a_ref[blk, :])
        etop = dot(inv, e_ref[blk, :])
        a_ref[...] = a_ref[...] - dot(left, top)
        e_ref[...] = e_ref[...] - dot(left, etop)
        a_ref[blk, :] = top
        e_ref[blk, :] = etop
        a_ref[blk, blk] = d_ref[...]
        return 0
    lax.fori_loop(0, n // B, step, 0)
    upper = lax.broadcasted_iota(jnp.int32, (n, n), 0) <= lax.broadcasted_iota(jnp.int32, (n, n), 1)
    a_ref[...] = jnp.where(upper, a_ref[...], 0.0)


PEERS = ((1, 0), (3, 0), (2, 0), (1, 1), (3, 1), (2, 1), (0, 1))
NEAR = ((1, 0), (3, 0), (1, 1), (3, 1))


def rows_of(start, size, unit):
    return pl.ds(pl.multiple_of(start, unit), size)


def kernel(ct_hbm, s_hbm, v_hbm, ft, wh, pr,
           ct, cr, s, v, vt, square, a, e, d, f, y, zv, own, other,
           load_sem, top_s, top_r, col_s, col_r, vec_s, vec_r, back_s, back_r):
    width, length = ct.shape
    n = square.shape[0]
    span = v.shape[0]
    half = span // 2
    nh = n // 2
    row, col = lax.axis_index("row"), lax.axis_index("col")
    lo, core = row // 2, row % 2
    z = col * 2 + lo
    member = row * 2 + col

    def place(dz, dc):
        zz, cc = (z + dz) % 4, (core + dc) % 2
        return (zz % 2) * 2 + cc, zz // 2

    def peer(dz, dc):
        r, c = place(dz, dc)
        return {"row": r, "col": c}

    def remote(src, dst, send, recv, to):
        return pltpu.make_async_remote_copy(
            src_ref=src, dst_ref=dst, send_sem=send, recv_sem=recv, device_id=to, device_id_type=MESH
        )

    mine = rows_of(member * width, width, 8)
    top_load = pltpu.make_async_copy(ct_hbm.at[:, pl.ds(0, n)], square.at[mine, :], load_sem.at[0])
    ct_load = pltpu.make_async_copy(ct_hbm, ct, load_sem.at[1])
    cr_load = pltpu.make_async_copy(
        ct_hbm.at[:, rows_of(row * span, span, 128)], cr.at[mine, :], load_sem.at[2]
    )
    s_load = pltpu.make_async_copy(s_hbm, s, load_sem.at[3])
    v_load = pltpu.make_async_copy(v_hbm, v, load_sem.at[4])
    for load in (top_load, ct_load, cr_load, v_load, s_load):
        load.start()

    barrier = pltpu.get_barrier_semaphore()
    for dz, dc in PEERS:
        pl.semaphore_signal(barrier, inc=1, device_id=peer(dz, dc), device_id_type=MESH)
    pl.semaphore_wait(barrier, len(PEERS))

    top_load.wait()
    tops = []
    for i, (dz, dc) in enumerate(PEERS):
        copy = remote(square.at[mine, :], square.at[mine, :], top_s.at[i], top_r.at[i], peer(dz, dc))
        copy.start()
        tops.append(copy)
    ct_load.wait()
    cols = []
    for i, (dz, dc) in enumerate(PEERS):
        r, _ = place(dz, dc)
        copy = remote(
            ct.at[:, rows_of(r * span, span, 128)], cr.at[mine, :], col_s.at[i], col_r.at[i], peer(dz, dc)
        )
        copy.start()
        cols.append(copy)

    v_load.wait()
    first, second = pl.ds(0, nh), pl.ds(nh, nh)
    to_core = remote(v.at[pl.ds(0, n), :], vt, vec_s.at[0], vec_r.at[0], {"row": 1, "col": col})
    to_first = remote(v.at[first, :], vt.at[first, :], vec_s.at[1], vec_r.at[1], {"row": 2, "col": col})
    to_second = remote(v.at[second, :], vt.at[second, :], vec_s.at[2], vec_r.at[1], {"row": 3, "col": col})
    pass_first = remote(vt.at[first, :], vt.at[first, :], vec_s.at[0], vec_r.at[0], {"row": 3, "col": col})
    pass_second = remote(vt.at[second, :], vt.at[second, :], vec_s.at[0], vec_r.at[0], {"row": 2, "col": col})

    @pl.when(row == 0)
    def _():
        to_core.start()
        to_first.start()
        to_second.start()
        vt[...] = v[pl.ds(0, n), :]

    for copy in tops:
        copy.wait()
    a[...] = square[...]
    factor(a, e, d, f)
    inverse = e[...]

    s_load.wait()
    wh[...] = dot(inverse, s[...])

    @pl.when(row == 2)
    def _():
        to_first.wait_recv()
        pass_first.start()
        pass_second.wait_recv()

    @pl.when(row == 3)
    def _():
        to_second.wait_recv()
        pass_second.start()
        pass_first.wait_recv()

    @pl.when(row == 1)
    def _():
        to_core.wait_recv()

    y[...] = dot(inverse, vt[...])
    zv[...] = dot(inverse.T, y[...])

    cr_load.wait()
    for copy in cols:
        copy.wait_recv()
    block = rows_of(row * span + col * half, half, 128)
    other[...] = dot(e[rows_of((1 - lo) * nh, nh, 8), :], cr[:, rows_of(col * half, half, 128)])
    backs = []
    for i, (dz, dc) in enumerate(NEAR):
        r, c = place(dz, dc)
        copy = remote(
            other.at[rows_of((r % 2) * 2 * width + c * width, width, 8), :],
            ft.at[:, block], back_s.at[i], back_r.at[i], peer(dz, dc),
        )
        copy.start()
        backs.append(copy)
    for j in range(2):
        rows = rows_of(((lo * 2 + (core + j) % 2) * 2 + col) * width, width, 8)
        own[pl.ds(j * width, width), :] = e[rows, :]
    kept = dot(own[...], cr[...])
    ft[:, rows_of(row * span, span, 128)] = kept[:width]
    give_ref = ct
    for copy in cols:
        copy.wait_send()
    give_ref[:, pl.ds(0, span)] = kept[width:]
    copy = remote(
        give_ref.at[:, pl.ds(0, span)], ft.at[:, rows_of(row * span, span, 128)],
        back_s.at[4], back_r.at[4], peer(0, 1),
    )
    copy.start()
    backs.append(copy)

    step = 256

    def project(i, _):
        part = rows_of(i * step, step, 128)
        pr[part, :] = v[part, :] - dot(cr[:, part].T, zv[...])
        return 0

    lax.fori_loop(0, span // step, project, 0)

    @pl.when(row == 0)
    def _():
        to_core.wait_send()
        to_first.wait_send()
        to_second.wait_send()
        pr[pl.ds(0, n), :] = y[...]

    @pl.when(row == 2)
    def _():
        pass_first.wait_send()

    @pl.when(row == 3)
    def _():
        pass_second.wait_send()

    for copy in backs:
        copy.wait()
    ft[:, pl.ds(0, n)] = a[mine, :]


def shards(foreground_cols, signal_rows, visibilities):
    length, width = foreground_cols.shape
    n = signal_rows.shape[0]
    span, vecs = visibilities.shape
    vmem = pl.BlockSpec(memory_space=pltpu.VMEM)
    hbm = pl.BlockSpec(memory_space=pl.ANY)
    dma = pltpu.SemaphoreType.DMA
    buffers = (
        (width, length), (n, span), signal_rows.shape, visibilities.shape, (n, vecs), (n, n), (n, n), (n, n),
        (B, B), (B, B), (n, vecs), (n, vecs), (2 * width, n), (n // 2, span // 2),
    )
    ft, whitened, projected = pl.pallas_call(
        kernel,
        name="whiten",
        out_shape=[
            jax.ShapeDtypeStruct((width, length), F32),
            jax.ShapeDtypeStruct(signal_rows.shape, F32),
            jax.ShapeDtypeStruct(visibilities.shape, F32),
        ],
        in_specs=[hbm] * 3,
        out_specs=[vmem] * 3,
        scratch_shapes=[pltpu.VMEM(shape, F32) for shape in buffers]
        + [dma((k,)) for k in (5, 7, 7, 7, 7, 3, 2, 5, 5)],
        compiler_params=pltpu.CompilerParams(
            collective_id=0, has_side_effects=True, vmem_limit_bytes=60 * 1024 * 1024
        ),
    )(foreground_cols.T, signal_rows, visibilities)
    return ft.T, whitened, projected


def solution(mesh):
    return jax.shard_map(
        shards,
        mesh=mesh,
        in_specs=(P("ma", ("row", "col")), P("ma", ("row", "col")), P(("ma", "row"), "col")),
        out_specs=(P("ma", ("row", "col")), P("ma", ("row", "col")), P(("ma", "row"), "col")),
        check_vma=False,
    )
```

time: 250 us -> 86.1 us (0.34)
  other arithmetic: 91.5 us -> 0 us
  Pallas kernels: 0 us -> 77.8 us
  blocking collectives: 41.4 us -> 0 us
  waiting for transfers between devices: 36.1 us -> 0 us
  matrix products: 28.5 us -> 0 us
  between operations: 16.3 us -> 0.65 us
  starting transfers between devices: 14.8 us -> 0 us
  local copies, waits for them, and re-layouts: 21.1 us -> 7.55 us
    another operation x15 -> x0, other arithmetic: 89.8 us -> none  [the longest x10 56.4 us: rows_layout(): top_factor = jnp.linalg.cholesky(top_square)]
    pallas_call x0 -> x1, Pallas kernels: none -> 77.8 us  [shards(): pl.pallas_call(kernel, name='whiten', out_shape=[jax.ShapeDtypeStruct((wi...]
    all_to_all x1 -> x0, blocking collectives: 41.4 us -> none  [rows_layout(): lax.all_to_all(lower_rows, ('row', 'col'), split_axis=1, concat_axis=0, t...]
    all_to_all x3 -> x0, waiting for transfers between devices: 36.1 us -> none  [the longest x2 36.1 us: from_everyone(): return lax.all_to_all(copies, axis, split_axis=0, concat_axis=0, tiled=True)]
    another operation x19 -> x0, matrix products: 16.3 us -> none  [the longest x5 6.43 us: rows_layout(): lax.linalg.triangular_solve(top_factor, signal_rows, left_side=True, lowe...]
    all_to_all x3 -> x0, starting transfers between devices: 14.8 us -> none  [the longest x2 11 us: from_everyone(): return lax.all_to_all(copies, axis, split_axis=0, concat_axis=0, tiled=True)]
    dot_general x1 -> x0, matrix products: 12.3 us -> none  [rows_layout(): jnp.dot(own_rows, head_solved, precision=lax.Precision.HIGHEST)]
    another operation x17 -> x0, local copies, waits for them, and re-layouts: 9.17 us -> none
  transfers between devices with their start and end apart: 4 -> 0, of which waited for: 2 -> 0; matrix products, arithmetic and copies ran while one was open for 49% -> 0% of each run, Pallas kernels for 0% -> 0%
where the time goes in v1:
time: 86.1 us; the launch traced here: 86 us
  Pallas kernels  77.8 us (90%)
  local copies, waits for them, and re-layouts  7.55 us (9%)
    pallas_call x1, Pallas kernels, shards(): pl.pallas_call(kernel, name='whiten', out_shape=[jax.ShapeDtypeStruct((wi...  77.8 us
    unnamed x5, local copies, waits for them, and re-layouts  7.55 us

profile of v1, /device:TPU:1, one launch (start us, length us, event | category | flops | bytes accessed | tf_op | source)
XLA Modules:
  0.0 86.0 jit_solution(16212183965976553953)
XLA Ops:
  0.6 77.8 %whiten.1 = (f32[48,8192]{1,0:T(8,128)}, f32[384,1024]{1,0:T(8,128)}, f32[2048,512]{1,0:T(8,128)}) custom-call(f32[48,8192]{1,0:T(8,128)} %bitcast.2, f32[384,1024]{1,0:T(8,128)} %s_hbm.1, f32[2048,512]{1,0:T(8,128)} %v_hbm.1), custom_call_target="tpu_custom_call" | custom-call | tf_op jit(solution)/shard_map/whiten/pallas_call | solution.py:260
  78.4 0.0 copy-start
  78.4 2.8 %copy.9 = f32[8192,48]{0,1:T(8,128)} copy(f32[8192,48]{0,1:T(8,128)} %bitcast.3) | data formatting | bytes 3145728
  81.2 2.7 %copy.10 = f32[384,1024]{1,0:T(8,128)} copy(f32[384,1024]{1,0:T(8,128)} %get-tuple-element.13) | data formatting | bytes 3145728
  84.0 0.0 copy-done
  84.0 2.0 %copy.11 = f32[2048,512]{1,0:T(8,128)} copy(f32[2048,512]{1,0:T(8,128)S(1)} %copy-done) | data formatting | bytes 8388608
Async XLA Ops:
  78.4 5.5 %copy-start = (f32[2048,512]{1,0:T(8,128)S(1)}, f32[2048,512]{1,0:T(8,128)}, u32[]{:S(2)}) copy-start(f32[2048,512]{1,0:T(8,128)} %get-tuple-element.14) | copy-start | bytes 12582916

commit v2 on v1

--- a/solution.py
+++ b/solution.py
@@ -79,6 +79,7 @@
 
 
 PEERS = ((1, 0), (3, 0), (2, 0), (1, 1), (3, 1), (2, 1), (0, 1))
+FAR = ((1, 0), (3, 0), (2, 0))
 NEAR = ((1, 0), (3, 0), (1, 1), (3, 1))
 
 
@@ -87,8 +88,8 @@
 
 
 def kernel(ct_hbm, s_hbm, v_hbm, ft, wh, pr,
-           ct, cr, s, v, vt, square, a, e, d, f, y, zv, own, other,
-           load_sem, top_s, top_r, col_s, col_r, vec_s, vec_r, back_s, back_r):
+           ct, cr, s, v, vt, square, a, e, d, f, y, zv, left, near, own,
+           load_sem, top_s, top_r, pass_s, pass_r, col_s, col_r, vec_s, vec_r, back_s, back_r):
     width, length = ct.shape
     n = square.shape[0]
     span = v.shape[0]
@@ -97,7 +98,6 @@
     row, col = lax.axis_index("row"), lax.axis_index("col")
     lo, core = row // 2, row % 2
     z = col * 2 + lo
-    member = row * 2 + col
 
     def place(dz, dc):
         zz, cc = (z + dz) % 4, (core + dc) % 2
@@ -106,20 +106,24 @@
     def peer(dz, dc):
         r, c = place(dz, dc)
         return {"row": r, "col": c}
+
+    def band(dz, dc):
+        r, c = place(dz, dc)
+        return rows_of((r * 2 + c) * width, width, 8)
 
     def remote(src, dst, send, recv, to):
         return pltpu.make_async_remote_copy(
             src_ref=src, dst_ref=dst, send_sem=send, recv_sem=recv, device_id=to, device_id_type=MESH
         )
 
-    mine = rows_of(member * width, width, 8)
+    mine = band(0, 0)
     top_load = pltpu.make_async_copy(ct_hbm.at[:, pl.ds(0, n)], square.at[mine, :], load_sem.at[0])
     ct_load = pltpu.make_async_copy(ct_hbm, ct, load_sem.at[1])
     cr_load = pltpu.make_async_copy(
         ct_hbm.at[:, rows_of(row * span, span, 128)], cr.at[mine, :], load_sem.at[2]
     )
-    s_load = pltpu.make_async_copy(s_hbm, s, load_sem.at[3])
-    v_load = pltpu.make_async_copy(v_hbm, v, load_sem.at[4])
+    v_load = pltpu.make_async_copy(v_hbm, v, load_sem.at[3])
+    s_load = pltpu.make_async_copy(s_hbm, s, load_sem.at[4])
     for load in (top_load, ct_load, cr_load, v_load, s_load):
         load.start()
 
@@ -129,20 +133,30 @@
     pl.semaphore_wait(barrier, len(PEERS))
 
     top_load.wait()
-    tops = []
-    for i, (dz, dc) in enumerate(PEERS):
-        copy = remote(square.at[mine, :], square.at[mine, :], top_s.at[i], top_r.at[i], peer(dz, dc))
+    tops, passes = [], []
+    for i, (dz, dc) in enumerate(FAR):
+        tops.append(remote(square.at[mine, :], square.at[mine, :], top_s.at[i], top_r.at[i], peer(dz, dc)))
+    for i, (dz, dc) in enumerate(FAR + ((0, 0),)):
+        block = square.at[band(-dz, dc), :]
+        passes.append(remote(block, block, pass_s.at[i], pass_r.at[i], peer(0, 1)))
+    for copy in tops:
         copy.start()
-        tops.append(copy)
+    passes[3].start()
+
     ct_load.wait()
-    cols = []
-    for i, (dz, dc) in enumerate(PEERS):
-        r, _ = place(dz, dc)
-        copy = remote(
-            ct.at[:, rows_of(r * span, span, 128)], cr.at[mine, :], col_s.at[i], col_r.at[i], peer(dz, dc)
-        )
+    cols = [[], []]
+    for turn in range(2):
+        for i, (dz, dc) in enumerate(PEERS):
+            r, c = place(dz, dc)
+            which = c if turn == 0 else 1 - c
+            copy = remote(
+                ct.at[:, rows_of(r * span + which * half, half, 128)],
+                cr.at[mine, rows_of(which * half, half, 128)],
+                col_s.at[turn, i], col_r.at[turn, i], peer(dz, dc),
+            )
+            cols[turn].append(copy)
+    for copy in cols[0]:
         copy.start()
-        cols.append(copy)
 
     v_load.wait()
     first, second = pl.ds(0, nh), pl.ds(nh, nh)
@@ -159,8 +173,16 @@
         to_second.start()
         vt[...] = v[pl.ds(0, n), :]
 
+    for copy in cols[1]:
+        copy.start()
+
+    for i in range(3):
+        tops[i].wait_recv()
+        passes[i].start()
+    for copy in passes:
+        copy.wait()
     for copy in tops:
-        copy.wait()
+        copy.wait_send()
     a[...] = square[...]
     factor(a, e, d, f)
     inverse = e[...]
@@ -184,47 +206,58 @@
     def _():
         to_core.wait_recv()
 
-    y[...] = dot(inverse, vt[...])
-    zv[...] = dot(inverse.T, y[...])
+    left[pl.ds(0, nh), :] = e[rows_of((1 - lo) * nh, nh, 8), :]
+    for j in range(2):
+        left[pl.ds(nh + j * width, width), :] = e[band(0, j), :]
 
     cr_load.wait()
-    for copy in cols:
+    for copy in cols[0]:
         copy.wait_recv()
-    block = rows_of(row * span + col * half, half, 128)
-    other[...] = dot(e[rows_of((1 - lo) * nh, nh, 8), :], cr[:, rows_of(col * half, half, 128)])
+    here, there = rows_of(col * half, half, 128), rows_of((1 - col) * half, half, 128)
+    here_out = rows_of(row * span + col * half, half, 128)
+    there_out = rows_of(row * span + (1 - col) * half, half, 128)
+    near[...] = dot(left[pl.ds(0, nh), :], cr[:, here])
     backs = []
     for i, (dz, dc) in enumerate(NEAR):
         r, c = place(dz, dc)
         copy = remote(
-            other.at[rows_of((r % 2) * 2 * width + c * width, width, 8), :],
-            ft.at[:, block], back_s.at[i], back_r.at[i], peer(dz, dc),
+            near.at[rows_of((r % 2) * 2 * width + c * width, width, 8), :],
+            ft.at[:, here_out], back_s.at[i], back_r.at[i], peer(dz, dc),
         )
         copy.start()
         backs.append(copy)
-    for j in range(2):
-        rows = rows_of(((lo * 2 + (core + j) % 2) * 2 + col) * width, width, 8)
-        own[pl.ds(j * width, width), :] = e[rows, :]
-    kept = dot(own[...], cr[...])
-    ft[:, rows_of(row * span, span, 128)] = kept[:width]
-    give_ref = ct
-    for copy in cols:
-        copy.wait_send()
-    give_ref[:, pl.ds(0, span)] = kept[width:]
-    copy = remote(
-        give_ref.at[:, pl.ds(0, span)], ft.at[:, rows_of(row * span, span, 128)],
-        back_s.at[4], back_r.at[4], peer(0, 1),
-    )
+    kept = dot(left[pl.ds(nh, 2 * width), :], cr[:, here])
+    ft[:, here_out] = kept[:width]
+    own[0, :, :] = kept[width:]
+    copy = remote(own.at[0], ft.at[:, here_out], back_s.at[4], back_r.at[4], peer(0, 1))
     copy.start()
     backs.append(copy)
 
+    y[...] = dot(inverse, vt[...])
+    zv[...] = dot(inverse.T, y[...])
+
     step = 256
 
-    def project(i, _):
-        part = rows_of(i * step, step, 128)
-        pr[part, :] = v[part, :] - dot(cr[:, part].T, zv[...])
-        return 0
-
-    lax.fori_loop(0, span // step, project, 0)
+    def project(start):
+        def body(i, _):
+            part = rows_of(start + i * step, step, 128)
+            pr[part, :] = v[part, :] - dot(cr[:, part].T, zv[...])
+            return 0
+
+        lax.fori_loop(0, half // step, body, 0)
+
+    project(col * half)
+
+    for copy in cols[1]:
+        copy.wait_recv()
+    kept = dot(left[pl.ds(nh, 2 * width), :], cr[:, there])
+    ft[:, there_out] = kept[:width]
+    own[1, :, :] = kept[width:]
+    copy = remote(own.at[1], ft.at[:, there_out], back_s.at[5], back_r.at[5], peer(0, 1))
+    copy.start()
+    backs.append(copy)
+
+    project((1 - col) * half)
 
     @pl.when(row == 0)
     def _():
@@ -241,6 +274,8 @@
     def _():
         pass_second.wait_send()
 
+    for copy in cols[0] + cols[1]:
+        copy.wait_send()
     for copy in backs:
         copy.wait()
     ft[:, pl.ds(0, n)] = a[mine, :]
@@ -255,22 +290,22 @@
     dma = pltpu.SemaphoreType.DMA
     buffers = (
         (width, length), (n, span), signal_rows.shape, visibilities.shape, (n, vecs), (n, n), (n, n), (n, n),
-        (B, B), (B, B), (n, vecs), (n, vecs), (2 * width, n), (n // 2, span // 2),
+        (B, B), (B, B), (n, vecs), (n, vecs), (n // 2 + 2 * width, n), (n // 2, span // 2), (2, width, span // 2),
     )
     ft, whitened, projected = pl.pallas_call(
         kernel,
         name="whiten",
         out_shape=[
-            jax.ShapeDtypeStruct((width, length), F32),
-            jax.ShapeDtypeStruct(signal_rows.shape, F32),
-            jax.ShapeDtypeStruct(visibilities.shape, F32),
+            pltpu.VMEM((width, length), F32),
+            pltpu.VMEM(signal_rows.shape, F32),
+            pltpu.VMEM(visibilities.shape, F32),
         ],
         in_specs=[hbm] * 3,
         out_specs=[vmem] * 3,
         scratch_shapes=[pltpu.VMEM(shape, F32) for shape in buffers]
-        + [dma((k,)) for k in (5, 7, 7, 7, 7, 3, 2, 5, 5)],
+        + [dma(k) for k in ((5,), (3,), (3,), (4,), (4,), (2, 7), (2, 7), (3,), (2,), (6,), (6,))],
         compiler_params=pltpu.CompilerParams(
-            collective_id=0, has_side_effects=True, vmem_limit_bytes=60 * 1024 * 1024
+            collective_id=0, has_side_effects=True, vmem_limit_bytes=56 * 1024 * 1024
         ),
     )(foreground_cols.T, signal_rows, visibilities)
     return ft.T, whitened, projected

time: 86.1 us -> 68 us (0.79)
  Pallas kernels: 77.8 us -> 62.9 us
  local copies, waits for them, and re-layouts: 7.55 us -> 4.3 us
    pallas_call x1, Pallas kernels: 77.8 us -> 62.9 us  [shards(): pl.pallas_call(kernel, name='whiten', out_shape=[pltpu.VMEM((width, lengt...]
    unnamed x5 -> x3, local copies, waits for them, and re-layouts: 7.55 us -> 4.3 us
where the time goes in v2:
time: 68 us; the launch traced here: 67.9 us
  Pallas kernels  62.9 us (92%)
  local copies, waits for them, and re-layouts  4.3 us (6%)
    pallas_call x1, Pallas kernels, shards(): pl.pallas_call(kernel, name='whiten', out_shape=[pltpu.VMEM((width, lengt...  62.9 us
    unnamed x3, local copies, waits for them, and re-layouts  4.3 us

profile of v2, /device:TPU:1, one launch (start us, length us, event | category | flops | bytes accessed | tf_op | source)
XLA Modules:
  0.0 67.9 jit_solution(12770367651254564180)
XLA Ops:
  0.6 62.9 %whiten.1 = (f32[48,8192]{1,0:T(8,128)S(1)}, f32[384,1024]{1,0:T(8,128)S(1)}, f32[2048,512]{1,0:T(8,128)S(1)}) custom-call(f32[48,8192]{1,0:T(8,128)} %bitcast.3, f32[384,1024]{1,0:T(8,128)} %s_hbm.1, f32[2048,512]{1,0:T(8,128)} %v_hbm.1), custom_call_target="tpu_custom_call" | custom-call | tf_op jit(solution)/shard_map/whiten/pallas_call | solution.py:295
  63.6 1.1 %copy.9 = f32[8192,48]{0,1:T(8,128)} copy(f32[8192,48]{0,1:T(8,128)S(1)} %bitcast.2) | data formatting | bytes 3145728
  64.7 1.1 %copy.10 = f32[384,1024]{1,0:T(8,128)} copy(f32[384,1024]{1,0:T(8,128)S(1)} %get-tuple-element.10) | data formatting | bytes 3145728
  65.9 2.0 %copy.11 = f32[2048,512]{1,0:T(8,128)} copy(f32[2048,512]{1,0:T(8,128)S(1)} %get-tuple-element.11) | data formatting | bytes 8388608

commit v3 on v2

--- a/solution.py
+++ b/solution.py
@@ -80,16 +80,27 @@
 
 PEERS = ((1, 0), (3, 0), (2, 0), (1, 1), (3, 1), (2, 1), (0, 1))
 FAR = ((1, 0), (3, 0), (2, 0))
-NEAR = ((1, 0), (3, 0), (1, 1), (3, 1))
 
 
 def rows_of(start, size, unit):
     return pl.ds(pl.multiple_of(start, unit), size)
 
 
+def split(x):
+    high = x.astype(jnp.bfloat16)
+    return high, (x - high.astype(F32)).astype(jnp.bfloat16)
+
+
+def dot3(a, b):
+    def one(x, y):
+        return lax.dot_general(x, y, (((1,), (0,)), ((), ())), preferred_element_type=F32)
+
+    return one(a[0], b[0]) + (one(a[0], b[1]) + one(a[1], b[0]))
+
+
 def kernel(ct_hbm, s_hbm, v_hbm, ft, wh, pr,
            ct, cr, s, v, vt, square, a, e, d, f, y, zv, left, near, own,
-           load_sem, top_s, top_r, pass_s, pass_r, col_s, col_r, vec_s, vec_r, back_s, back_r):
+           load_sem, top_s, top_r, pass_s, pass_r, col_s, col_r, vec_s, vec_r, back_s, back_r, give_s, give_r):
     width, length = ct.shape
     n = square.shape[0]
     span = v.shape[0]
@@ -144,17 +155,17 @@
     passes[3].start()
 
     ct_load.wait()
-    cols = [[], []]
-    for turn in range(2):
+    quarter = half // 2
+    cols = [[], [], []]
+    for turn, size in enumerate((half, quarter, quarter)):
         for i, (dz, dc) in enumerate(PEERS):
             r, c = place(dz, dc)
-            which = c if turn == 0 else 1 - c
-            copy = remote(
-                ct.at[:, rows_of(r * span + which * half, half, 128)],
-                cr.at[mine, rows_of(which * half, half, 128)],
+            early = (r // 2) * c
+            start = early * half if turn == 0 else (1 - early) * half + (turn - 1) * quarter
+            cols[turn].append(remote(
+                ct.at[:, rows_of(r * span + start, size, 128)], cr.at[mine, rows_of(start, size, 128)],
                 col_s.at[turn, i], col_r.at[turn, i], peer(dz, dc),
-            )
-            cols[turn].append(copy)
+            ))
     for copy in cols[0]:
         copy.start()
 
@@ -173,7 +184,7 @@
         to_second.start()
         vt[...] = v[pl.ds(0, n), :]
 
-    for copy in cols[1]:
+    for copy in cols[1] + cols[2]:
         copy.start()
 
     for i in range(3):
@@ -185,10 +196,64 @@
         copy.wait_send()
     a[...] = square[...]
     factor(a, e, d, f)
-    inverse = e[...]
+    left[pl.ds(0, nh), :] = e[rows_of((1 - lo) * nh, nh, 8), :]
+    for j in range(2):
+        left[pl.ds(nh + j * width, width), :] = e[band(0, j), :]
+
+    cr_load.wait()
+    for copy in cols[0]:
+        copy.wait_recv()
+    early = lo * col
+    base = row * span
+    lefts = split(left[...])
+    def back(dz, dc, kind, start, size):
+        r, c = place(dz, dc)
+        return remote(
+            near.at[rows_of((r % 2) * 2 * width + c * width, width, 8), rows_of(start, size, 128)],
+            ft.at[:, rows_of(base + start, size, 128)],
+            back_s.at[kind, dc], back_r.at[kind, dc], peer(dz, dc),
+        )
+
+    short = [back(1, dc, 0, n, quarter - n) for dc in range(2)]
+    full = [back(1, dc, 0, 0, quarter) for dc in range(2)]
+    even = [back(3, dc, 1, quarter, quarter) for dc in range(2)]
+    rest = [[back(3, dc, kind, kind * quarter, quarter) for dc in range(2)] for kind in (2, 3)]
+    odd = [back(dz, dc, kind, col * half, half) for dc in range(2) for dz, kind in ((1, 0), (3, 1))]
+
+    def on_kind(step):
+        @pl.when(row == 0)
+        def _():
+            for copy in short + even:
+                step(copy)
+
+        @pl.when(row == 1)
+        def _():
+            for copy in full + even:
+                step(copy)
+
+        @pl.when(lo == 1)
+        def _():
+            for copy in odd:
+                step(copy)
+
+    given = []
+
+    def factor_rows(slot, start, size):
+        lanes, out = rows_of(start, size, 128), rows_of(base + start, size, 128)
+        got = dot3(lefts, split(cr[:, lanes]))
+        near[:, lanes] = got[:nh]
+        ft[:, out] = got[nh:nh + width]
+        own[:, lanes] = got[nh + width:]
+        copy = remote(own.at[:, lanes], ft.at[:, out], give_s.at[slot], give_r.at[slot], peer(0, 1))
+        copy.start()
+        given.append(copy)
+
+    factor_rows(0, early * half, half)
+    on_kind(lambda copy: copy.start())
 
     s_load.wait()
-    wh[...] = dot(inverse, s[...])
+    inverse = split(e[...])
+    wh[...] = dot3(inverse, split(s[...]))
 
     @pl.when(row == 2)
     def _():
@@ -206,58 +271,32 @@
     def _():
         to_core.wait_recv()
 
-    left[pl.ds(0, nh), :] = e[rows_of((1 - lo) * nh, nh, 8), :]
-    for j in range(2):
-        left[pl.ds(nh + j * width, width), :] = e[band(0, j), :]
-
-    cr_load.wait()
-    for copy in cols[0]:
-        copy.wait_recv()
-    here, there = rows_of(col * half, half, 128), rows_of((1 - col) * half, half, 128)
-    here_out = rows_of(row * span + col * half, half, 128)
-    there_out = rows_of(row * span + (1 - col) * half, half, 128)
-    near[...] = dot(left[pl.ds(0, nh), :], cr[:, here])
-    backs = []
-    for i, (dz, dc) in enumerate(NEAR):
-        r, c = place(dz, dc)
-        copy = remote(
-            near.at[rows_of((r % 2) * 2 * width + c * width, width, 8), :],
-            ft.at[:, here_out], back_s.at[i], back_r.at[i], peer(dz, dc),
-        )
-        copy.start()
-        backs.append(copy)
-    kept = dot(left[pl.ds(nh, 2 * width), :], cr[:, here])
-    ft[:, here_out] = kept[:width]
-    own[0, :, :] = kept[width:]
-    copy = remote(own.at[0], ft.at[:, here_out], back_s.at[4], back_r.at[4], peer(0, 1))
-    copy.start()
-    backs.append(copy)
-
-    y[...] = dot(inverse, vt[...])
-    zv[...] = dot(inverse.T, y[...])
+    y[...] = dot3(inverse, split(vt[...]))
+    zv[...] = dot3(split(e[...].T), split(y[...]))
 
     step = 256
 
-    def project(start):
-        def body(i, _):
+    zs = split(zv[...])
+
+    def project(start, size):
+        for i in range(size // step):
             part = rows_of(start + i * step, step, 128)
-            pr[part, :] = v[part, :] - dot(cr[:, part].T, zv[...])
-            return 0
-
-        lax.fori_loop(0, half // step, body, 0)
-
-    project(col * half)
-
-    for copy in cols[1]:
-        copy.wait_recv()
-    kept = dot(left[pl.ds(nh, 2 * width), :], cr[:, there])
-    ft[:, there_out] = kept[:width]
-    own[1, :, :] = kept[width:]
-    copy = remote(own.at[1], ft.at[:, there_out], back_s.at[5], back_r.at[5], peer(0, 1))
-    copy.start()
-    backs.append(copy)
-
-    project((1 - col) * half)
+            pr[part, :] = v[part, :] - dot3(split(cr[:, part].T), zs)
+
+    project(early * half, half)
+
+    for turn in (1, 2):
+        late = (1 - early) * half + (turn - 1) * quarter
+        for copy in cols[turn]:
+            copy.wait_recv()
+        factor_rows(turn, late, quarter)
+
+        @pl.when(lo == 0)
+        def _():
+            for copy in rest[turn - 1]:
+                copy.start()
+
+        project(late, quarter)
 
     @pl.when(row == 0)
     def _():
@@ -274,11 +313,44 @@
     def _():
         pass_second.wait_send()
 
-    for copy in cols[0] + cols[1]:
+    for copy in cols[0] + cols[1] + cols[2]:
         copy.wait_send()
-    for copy in backs:
+    on_kind(lambda copy: copy.wait_send())
+
+    @pl.when(lo == 0)
+    def _():
+        for copy in rest[0] + rest[1]:
+            copy.wait_send()
+        for copy in odd:
+            copy.wait_recv()
+
+    @pl.when(lo == 1)
+    def _():
+        @pl.when(core == 0)
+        def _():
+            short[0].wait_recv()
+            full[1].wait_recv()
+
+        @pl.when(core == 1)
+        def _():
+            full[0].wait_recv()
+            short[1].wait_recv()
+
+        for copy in even + rest[0] + rest[1]:
+            copy.wait_recv()
+
+    for copy in given:
         copy.wait()
     ft[:, pl.ds(0, n)] = a[mine, :]
+
+
+def store(*refs):
+    sems = refs[6]
+    copies = [pltpu.make_async_copy(refs[i], refs[3 + i], sems.at[i]) for i in range(3)]
+    for copy in copies:
+        copy.start()
+    for copy in copies:
+        copy.wait()
 
 
 def shards(foreground_cols, signal_rows, visibilities):
@@ -290,7 +362,7 @@
     dma = pltpu.SemaphoreType.DMA
     buffers = (
         (width, length), (n, span), signal_rows.shape, visibilities.shape, (n, vecs), (n, n), (n, n), (n, n),
-        (B, B), (B, B), (n, vecs), (n, vecs), (n // 2 + 2 * width, n), (n // 2, span // 2), (2, width, span // 2),
+        (B, B), (B, B), (n, vecs), (n, vecs), (n // 2 + 2 * width, n), (n // 2, span), (width, span),
     )
     ft, whitened, projected = pl.pallas_call(
         kernel,
@@ -303,11 +375,20 @@
         in_specs=[hbm] * 3,
         out_specs=[vmem] * 3,
         scratch_shapes=[pltpu.VMEM(shape, F32) for shape in buffers]
-        + [dma(k) for k in ((5,), (3,), (3,), (4,), (4,), (2, 7), (2, 7), (3,), (2,), (6,), (6,))],
+        + [dma(k) for k in ((5,), (3,), (3,), (4,), (4,), (3, 7), (3, 7), (3,), (2,), (4, 2), (4, 2), (3,), (3,))],
         compiler_params=pltpu.CompilerParams(
             collective_id=0, has_side_effects=True, vmem_limit_bytes=56 * 1024 * 1024
         ),
     )(foreground_cols.T, signal_rows, visibilities)
+    ft, whitened, projected = pl.pallas_call(
+        store,
+        name="store",
+        out_shape=[jax.ShapeDtypeStruct(x.shape, F32) for x in (ft, whitened, projected)],
+        in_specs=[vmem] * 3,
+        out_specs=[hbm] * 3,
+        scratch_shapes=[dma((3,))],
+        compiler_params=pltpu.CompilerParams(vmem_limit_bytes=1024 * 1024),
+    )(ft, whitened, projected)
     return ft.T, whitened, projected
 
 

time: 68 us -> 63.8 us (0.938)
  local copies, waits for them, and re-layouts: 4.3 us -> 0 us
    unnamed x3 -> x0, local copies, waits for them, and re-layouts: 4.3 us -> none
    pallas_call x0 -> x1, Pallas kernels: none -> 3.08 us  [shards(): pl.pallas_call(store, name='store', out_shape=[jax.ShapeDtypeStruct(x.sha...]
    pallas_call x1, Pallas kernels: 62.9 us -> 59.9 us  [shards(): pl.pallas_call(kernel, name='whiten', out_shape=[pltpu.VMEM((width, lengt...]
where the time goes in v3:
time: 63.8 us; the launch traced here: 63.6 us
  Pallas kernels  63 us (99%)
  between operations  0.64 us (1%)
    pallas_call x1, Pallas kernels, shards(): pl.pallas_call(kernel, name='whiten', out_shape=[pltpu.VMEM((width, lengt...  59.9 us
    pallas_call x1, Pallas kernels, shards(): pl.pallas_call(store, name='store', out_shape=[jax.ShapeDtypeStruct(x.sha...  3.08 us

profile of v3, /device:TPU:1, one launch (start us, length us, event | category | flops | bytes accessed | tf_op | source)
XLA Modules:
  0.0 63.6 jit_solution(15011706045038461688)
XLA Ops:
  0.6 59.9 %whiten.1 = (f32[48,8192]{1,0:T(8,128)S(1)}, f32[384,1024]{1,0:T(8,128)S(1)}, f32[2048,512]{1,0:T(8,128)S(1)}) custom-call(f32[48,8192]{1,0:T(8,128)} %bitcast.2, f32[384,1024]{1,0:T(8,128)} %s_hbm.1, f32[2048,512]{1,0:T(8,128)} %v_hbm.1), custom_call_target="tpu_custom_call" | custom-call | tf_op jit(solution)/shard_map/whiten/pallas_call | solution.py:367
  60.6 3.1 %store.1 = (f32[48,8192]{1,0:T(8,128)}, f32[384,1024]{1,0:T(8,128)}, f32[2048,512]{1,0:T(8,128)}) custom-call(f32[48,8192]{1,0:T(8,128)S(1)} %get-tuple-element.9.refs_0_, f32[384,1024]{1,0:T(8,128)S(1)} %get-tuple-element.10.refs_1_, f32[2048,512]{1,0:T(8,128)S(1)} %get-tuple-element.11.refs_2_), custom_call_target="tpu_custom_call" | custom-call | tf_op jit(solution)/shard_map/store/pallas_call | solution.py:383

commit v4 on v3

--- a/solution.py
+++ b/solution.py
@@ -144,18 +144,41 @@
     pl.semaphore_wait(barrier, len(PEERS))
 
     top_load.wait()
-    tops, passes = [], []
-    for i, (dz, dc) in enumerate(FAR):
-        tops.append(remote(square.at[mine, :], square.at[mine, :], top_s.at[i], top_r.at[i], peer(dz, dc)))
-    for i, (dz, dc) in enumerate(FAR + ((0, 0),)):
-        block = square.at[band(-dz, dc), :]
-        passes.append(remote(block, block, pass_s.at[i], pass_r.at[i], peer(0, 1)))
-    for copy in tops:
-        copy.start()
-    passes[3].start()
+    def band_sizes(source_lo, step):
+        for when, size in ((source_lo == 1, n), (source_lo * 2 + core == 0, B), (source_lo * 2 + core == 1, 2 * B)):
+            @pl.when(when)
+            def _():
+                step(size)
+
+    def top(i, size):
+        block = square.at[mine, pl.ds(0, size)]
+        return remote(block, block, top_s.at[i], top_r.at[i], peer(*FAR[i]))
+
+    def top_in(i, size):
+        block = square.at[band(-FAR[i][0], 0), pl.ds(0, size)]
+        return remote(block, block, top_s.at[i], top_r.at[i], peer(*FAR[i]))
+
+    def handed(i, size):
+        block = square.at[band(-FAR[i][0] if i < 3 else 0, 0), pl.ds(0, size)]
+        return remote(block, block, pass_s.at[i], pass_r.at[i], peer(0, 1))
+
+    def got(i, size):
+        block = square.at[band(-FAR[i][0] if i < 3 else 0, 1), pl.ds(0, size)]
+        return remote(block, block, pass_s.at[i], pass_r.at[i], peer(0, 1))
+
+    def source(i):
+        return (lo + (FAR[i][0] if i < 3 else 0)) % 2
+
+    def start_tops(size):
+        for i in range(3):
+            top(i, size).start()
+        handed(3, size).start()
+
+    band_sizes(lo, start_tops)
 
     ct_load.wait()
     quarter = half // 2
+    cut = quarter + B
     cols = [[], [], []]
     for turn, size in enumerate((half, quarter, quarter)):
         for i, (dz, dc) in enumerate(PEERS):
@@ -166,8 +189,27 @@
                 ct.at[:, rows_of(r * span + start, size, 128)], cr.at[mine, rows_of(start, size, 128)],
                 col_s.at[turn, i], col_r.at[turn, i], peer(dz, dc),
             ))
-    for copy in cols[0]:
-        copy.start()
+    less = [
+        remote(
+            ct.at[:, pl.ds(n, half - n)], cr.at[mine, pl.ds(n, half - n)],
+            col_s.at[0, i], col_r.at[0, i], peer(dz, dc),
+        )
+        for i, (dz, dc) in enumerate(PEERS)
+    ]
+
+    def first_turn(step):
+        for i, (dz, dc) in enumerate(PEERS):
+            r, _ = place(dz, dc)
+
+            @pl.when(r == 0)
+            def _():
+                step(less[i])
+
+            @pl.when(r != 0)
+            def _():
+                step(cols[0][i])
+
+    first_turn(lambda copy: copy.start())
 
     v_load.wait()
     first, second = pl.ds(0, nh), pl.ds(nh, nh)
@@ -188,21 +230,56 @@
         copy.start()
 
     for i in range(3):
-        tops[i].wait_recv()
-        passes[i].start()
-    for copy in passes:
-        copy.wait()
-    for copy in tops:
-        copy.wait_send()
-    a[...] = square[...]
+        def forward(size, i=i):
+            top_in(i, size).wait_recv()
+            handed(i, size).start()
+
+        band_sizes(source(i), forward)
+
+    for i in range(4):
+        @pl.when(source(i) == 1)
+        def _():
+            got(i, n).wait_recv()
+
+        @pl.when((source(i) == 0) & (core == 1))
+        def _():
+            got(i, B).wait_recv()
+
+        @pl.when((source(i) == 0) & (core == 0))
+        def _():
+            got(i, 2 * B).wait_recv()
+
+        band_sizes(source(i), lambda size, i=i: handed(i, size).wait_send())
+
+    def end_tops(size):
+        for i in range(3):
+            top(i, size).wait_send()
+
+    band_sizes(lo, end_tops)
+    below = lax.broadcasted_iota(jnp.int32, (n, n), 0) >= lax.broadcasted_iota(jnp.int32, (n, n), 1)
+    a[...] = jnp.where(below, square[...], square[...].T)
+
+    cr_load.wait()
+
+    @pl.when(row == 0)
+    def _():
+        cr[:, pl.ds(0, n)] = a[...]
+
     factor(a, e, d, f)
     left[pl.ds(0, nh), :] = e[rows_of((1 - lo) * nh, nh, 8), :]
     for j in range(2):
         left[pl.ds(nh + j * width, width), :] = e[band(0, j), :]
 
-    cr_load.wait()
-    for copy in cols[0]:
-        copy.wait_recv()
+    @pl.when(row == 0)
+    def _():
+        for copy in less:
+            copy.wait_recv()
+
+    @pl.when(row != 0)
+    def _():
+        for copy in cols[0]:
+            copy.wait_recv()
+
     early = lo * col
     base = row * span
     lefts = split(left[...])
@@ -214,9 +291,9 @@
             back_s.at[kind, dc], back_r.at[kind, dc], peer(dz, dc),
         )
 
-    short = [back(1, dc, 0, n, quarter - n) for dc in range(2)]
-    full = [back(1, dc, 0, 0, quarter) for dc in range(2)]
-    even = [back(3, dc, 1, quarter, quarter) for dc in range(2)]
+    short = [back(1, dc, 0, n, cut - n) for dc in range(2)]
+    full = [back(1, dc, 0, 0, cut) for dc in range(2)]
+    even = [back(3, dc, 1, cut, half - cut) for dc in range(2)]
     rest = [[back(3, dc, kind, kind * quarter, quarter) for dc in range(2)] for kind in (2, 3)]
     odd = [back(dz, dc, kind, col * half, half) for dc in range(2) for dz, kind in ((1, 0), (3, 1))]
 
@@ -313,7 +390,8 @@
     def _():
         pass_second.wait_send()
 
-    for copy in cols[0] + cols[1] + cols[2]:
+    first_turn(lambda copy: copy.wait_send())
+    for copy in cols[1] + cols[2]:
         copy.wait_send()
     on_kind(lambda copy: copy.wait_send())
 

time: 63.8 us -> 61.1 us (0.958)
  Pallas kernels: 63 us -> 60.3 us
    pallas_call x1, Pallas kernels: 59.9 us -> 57.2 us  [shards(): pl.pallas_call(kernel, name='whiten', out_shape=[pltpu.VMEM((width, lengt...]
where the time goes in v4:
time: 61.1 us; the launch traced here: 60.9 us
  Pallas kernels  60.3 us (99%)
  between operations  0.64 us (1%)
    pallas_call x1, Pallas kernels, shards(): pl.pallas_call(kernel, name='whiten', out_shape=[pltpu.VMEM((width, lengt...  57.2 us
    pallas_call x1, Pallas kernels, shards(): pl.pallas_call(store, name='store', out_shape=[jax.ShapeDtypeStruct(x.sha...  3.08 us

profile of v4, /device:TPU:1, one launch (start us, length us, event | category | flops | bytes accessed | tf_op | source)
XLA Modules:
  0.0 60.9 jit_solution(6690898321777190810)
XLA Ops:
  0.6 57.2 %whiten.1 = (f32[48,8192]{1,0:T(8,128)S(1)}, f32[384,1024]{1,0:T(8,128)S(1)}, f32[2048,512]{1,0:T(8,128)S(1)}) custom-call(f32[48,8192]{1,0:T(8,128)} %bitcast.2, f32[384,1024]{1,0:T(8,128)} %s_hbm.1, f32[2048,512]{1,0:T(8,128)} %v_hbm.1), custom_call_target="tpu_custom_call" | custom-call | tf_op jit(solution)/shard_map/whiten/pallas_call | solution.py:445
  57.9 3.1 %store.1 = (f32[48,8192]{1,0:T(8,128)}, f32[384,1024]{1,0:T(8,128)}, f32[2048,512]{1,0:T(8,128)}) custom-call(f32[48,8192]{1,0:T(8,128)S(1)} %get-tuple-element.9.refs_0_, f32[384,1024]{1,0:T(8,128)S(1)} %get-tuple-element.10.refs_1_, f32[2048,512]{1,0:T(8,128)S(1)} %get-tuple-element.11.refs_2_), custom_call_target="tpu_custom_call" | custom-call | tf_op jit(solution)/shard_map/store/pallas_call | solution.py:461

commit v5 on v4

--- a/solution.py
+++ b/solution.py
@@ -209,13 +209,12 @@
             def _():
                 step(cols[0][i])
 
-    first_turn(lambda copy: copy.start())
 
     v_load.wait()
     first, second = pl.ds(0, nh), pl.ds(nh, nh)
     to_core = remote(v.at[pl.ds(0, n), :], vt, vec_s.at[0], vec_r.at[0], {"row": 1, "col": col})
     to_first = remote(v.at[first, :], vt.at[first, :], vec_s.at[1], vec_r.at[1], {"row": 2, "col": col})
-    to_second = remote(v.at[second, :], vt.at[second, :], vec_s.at[2], vec_r.at[1], {"row": 3, "col": col})
+    to_second = remote(vt.at[second, :], vt.at[second, :], vec_s.at[1], vec_r.at[1], {"row": 3, "col": col})
     pass_first = remote(vt.at[first, :], vt.at[first, :], vec_s.at[0], vec_r.at[0], {"row": 3, "col": col})
     pass_second = remote(vt.at[second, :], vt.at[second, :], vec_s.at[0], vec_r.at[0], {"row": 2, "col": col})
 
@@ -223,11 +222,23 @@
     def _():
         to_core.start()
         to_first.start()
+        vt[...] = v[pl.ds(0, n), :]
+
+    @pl.when(row == 1)
+    def _():
+        to_core.wait_recv()
         to_second.start()
-        vt[...] = v[pl.ds(0, n), :]
-
-    for copy in cols[1] + cols[2]:
-        copy.start()
+
+    first_turn(lambda copy: copy.start())
+    same = [i for i, (dz, _) in enumerate(PEERS) if dz % 2 == 0]
+    apart = [i for i, (dz, _) in enumerate(PEERS) if dz % 2 == 1]
+    for own_lo, order in ((0, (same, apart)), (1, (apart, same))):
+        @pl.when(lo == own_lo)
+        def _():
+            for group in order:
+                for turn in (1, 2):
+                    for i in group:
+                        cols[turn][i].start()
 
     for i in range(3):
         def forward(size, i=i):
@@ -266,6 +277,32 @@
         cr[:, pl.ds(0, n)] = a[...]
 
     factor(a, e, d, f)
+
+    @pl.when(row == 2)
+    def _():
+        to_first.wait_recv()
+        pass_first.start()
+
+    @pl.when(row == 3)
+    def _():
+        to_second.wait_recv()
+        pass_second.start()
+
+    s_load.wait()
+    inverse = split(e[...])
+    wh[...] = dot3(inverse, split(s[...]))
+
+    @pl.when(row == 2)
+    def _():
+        pass_second.wait_recv()
+
+    @pl.when(row == 3)
+    def _():
+        pass_first.wait_recv()
+
+    y[...] = dot3(inverse, split(vt[...]))
+    zv[...] = dot3(split(e[...].T), split(y[...]))
+
     left[pl.ds(0, nh), :] = e[rows_of((1 - lo) * nh, nh, 8), :]
     for j in range(2):
         left[pl.ds(nh + j * width, width), :] = e[band(0, j), :]
@@ -313,7 +350,9 @@
             for copy in odd:
                 step(copy)
 
-    given = []
+    def given(slot, start, size):
+        out = ft.at[:, rows_of(base + start, size, 128)]
+        return remote(own.at[:, rows_of(start, size, 128)], out, give_s.at[slot], give_r.at[slot], peer(0, 1))
 
     def factor_rows(slot, start, size):
         lanes, out = rows_of(start, size, 128), rows_of(base + start, size, 128)
@@ -321,66 +360,54 @@
         near[:, lanes] = got[:nh]
         ft[:, out] = got[nh:nh + width]
         own[:, lanes] = got[nh + width:]
-        copy = remote(own.at[:, lanes], ft.at[:, out], give_s.at[slot], give_r.at[slot], peer(0, 1))
-        copy.start()
-        given.append(copy)
+        given(slot, start, size).start()
 
     factor_rows(0, early * half, half)
     on_kind(lambda copy: copy.start())
 
-    s_load.wait()
-    inverse = split(e[...])
-    wh[...] = dot3(inverse, split(s[...]))
-
-    @pl.when(row == 2)
-    def _():
-        to_first.wait_recv()
-        pass_first.start()
-        pass_second.wait_recv()
-
-    @pl.when(row == 3)
-    def _():
-        to_second.wait_recv()
-        pass_second.start()
-        pass_first.wait_recv()
-
-    @pl.when(row == 1)
-    def _():
-        to_core.wait_recv()
-
-    y[...] = dot3(inverse, split(vt[...]))
-    zv[...] = dot3(split(e[...].T), split(y[...]))
-
     step = 256
 
     zs = split(zv[...])
 
     def project(start, size):
-        for i in range(size // step):
+        def one(i, _):
             part = rows_of(start + i * step, step, 128)
             pr[part, :] = v[part, :] - dot3(split(cr[:, part].T), zs)
-
-    project(early * half, half)
-
-    for turn in (1, 2):
-        late = (1 - early) * half + (turn - 1) * quarter
-        for copy in cols[turn]:
-            copy.wait_recv()
-        factor_rows(turn, late, quarter)
-
-        @pl.when(lo == 0)
-        def _():
+            return 0
+
+        lax.fori_loop(0, size // step, one, 0)
+
+    def late(turn):
+        return (1 - early) * half + (turn - 1) * quarter
+
+    @pl.when(lo == 0)
+    def _():
+        for turn in (1, 2):
+            for copy in cols[turn]:
+                copy.wait_recv()
+            factor_rows(turn, late(turn), quarter)
             for copy in rest[turn - 1]:
                 copy.start()
-
-        project(late, quarter)
+        project(0, span)
+
+    @pl.when(lo == 1)
+    def _():
+        project(early * half, half)
+        for turn in (1, 2):
+            for copy in cols[turn]:
+                copy.wait_recv()
+            factor_rows(turn, late(turn), quarter)
+            project(late(turn), quarter)
 
     @pl.when(row == 0)
     def _():
         to_core.wait_send()
         to_first.wait_send()
+        pr[pl.ds(0, n), :] = y[...]
+
+    @pl.when(row == 1)
+    def _():
         to_second.wait_send()
-        pr[pl.ds(0, n), :] = y[...]
 
     @pl.when(row == 2)
     def _():
@@ -417,8 +444,9 @@
         for copy in even + rest[0] + rest[1]:
             copy.wait_recv()
 
-    for copy in given:
-        copy.wait()
+    given(0, early * half, half).wait()
+    for turn in (1, 2):
+        given(turn, late(turn), quarter).wait()
     ft[:, pl.ds(0, n)] = a[mine, :]
 
 

time: 61.1 us -> 58.1 us (0.951)
  Pallas kernels: 60.3 us -> 57.4 us
    pallas_call x1, Pallas kernels: 57.2 us -> 54.3 us  [shards(): pl.pallas_call(kernel, name='whiten', out_shape=[pltpu.VMEM((width, lengt...]
where the time goes in v5:
time: 58.1 us; the launch traced here: 58 us
  Pallas kernels  57.4 us (99%)
  between operations  0.64 us (1%)
    pallas_call x1, Pallas kernels, shards(): pl.pallas_call(kernel, name='whiten', out_shape=[pltpu.VMEM((width, lengt...  54.3 us
    pallas_call x1, Pallas kernels, shards(): pl.pallas_call(store, name='store', out_shape=[jax.ShapeDtypeStruct(x.sha...  3.08 us

profile of v5, /device:TPU:1, one launch (start us, length us, event | category | flops | bytes accessed | tf_op | source)
XLA Modules:
  0.0 58.0 jit_solution(28911649438215564)
XLA Ops:
  0.6 54.3 %whiten.1 = (f32[48,8192]{1,0:T(8,128)S(1)}, f32[384,1024]{1,0:T(8,128)S(1)}, f32[2048,512]{1,0:T(8,128)S(1)}) custom-call(f32[48,8192]{1,0:T(8,128)} %bitcast.2, f32[384,1024]{1,0:T(8,128)} %s_hbm.1, f32[2048,512]{1,0:T(8,128)} %v_hbm.1), custom_call_target="tpu_custom_call" | custom-call | tf_op jit(solution)/shard_map/whiten/pallas_call | solution.py:473
  54.9 3.1 %store.1 = (f32[48,8192]{1,0:T(8,128)}, f32[384,1024]{1,0:T(8,128)}, f32[2048,512]{1,0:T(8,128)}) custom-call(f32[48,8192]{1,0:T(8,128)S(1)} %get-tuple-element.9.refs_0_, f32[384,1024]{1,0:T(8,128)S(1)} %get-tuple-element.10.refs_1_, f32[2048,512]{1,0:T(8,128)S(1)} %get-tuple-element.11.refs_2_), custom_call_target="tpu_custom_call" | custom-call | tf_op jit(solution)/shard_map/store/pallas_call | solution.py:489

commit v6 on v5

--- a/solution.py
+++ b/solution.py
@@ -178,7 +178,7 @@
 
     ct_load.wait()
     quarter = half // 2
-    cut = quarter + B
+    cut = quarter + 2 * B
     cols = [[], [], []]
     for turn, size in enumerate((half, quarter, quarter)):
         for i, (dz, dc) in enumerate(PEERS):

time: 58.1 us -> 57.4 us (0.988)
  Pallas kernels: 57.4 us -> 56.7 us
    pallas_call x1, Pallas kernels: 54.3 us -> 53.6 us  [shards(): pl.pallas_call(kernel, name='whiten', out_shape=[pltpu.VMEM((width, lengt...]
where the time goes in v6:
time: 57.4 us; the launch traced here: 57.3 us
  Pallas kernels  56.7 us (99%)
  between operations  0.64 us (1%)
    pallas_call x1, Pallas kernels, shards(): pl.pallas_call(kernel, name='whiten', out_shape=[pltpu.VMEM((width, lengt...  53.6 us
    pallas_call x1, Pallas kernels, shards(): pl.pallas_call(store, name='store', out_shape=[jax.ShapeDtypeStruct(x.sha...  3.08 us

profile of v6, /device:TPU:1, one launch (start us, length us, event | category | flops | bytes accessed | tf_op | source)
XLA Modules:
  0.0 57.3 jit_solution(6517234598565914284)
XLA Ops:
  0.6 53.6 %whiten.1 = (f32[48,8192]{1,0:T(8,128)S(1)}, f32[384,1024]{1,0:T(8,128)S(1)}, f32[2048,512]{1,0:T(8,128)S(1)}) custom-call(f32[48,8192]{1,0:T(8,128)} %bitcast.2, f32[384,1024]{1,0:T(8,128)} %s_hbm.1, f32[2048,512]{1,0:T(8,128)} %v_hbm.1), custom_call_target="tpu_custom_call" | custom-call | tf_op jit(solution)/shard_map/whiten/pallas_call | solution.py:473
  54.2 3.1 %store.1 = (f32[48,8192]{1,0:T(8,128)}, f32[384,1024]{1,0:T(8,128)}, f32[2048,512]{1,0:T(8,128)}) custom-call(f32[48,8192]{1,0:T(8,128)S(1)} %get-tuple-element.9.refs_0_, f32[384,1024]{1,0:T(8,128)S(1)} %get-tuple-element.10.refs_1_, f32[2048,512]{1,0:T(8,128)S(1)} %get-tuple-element.11.refs_2_), custom_call_target="tpu_custom_call" | custom-call | tf_op jit(solution)/shard_map/store/pallas_call | solution.py:489

commit v7 on v6

--- a/solution.py
+++ b/solution.py
@@ -197,9 +197,9 @@
         for i, (dz, dc) in enumerate(PEERS)
     ]
 
-    def first_turn(step):
-        for i, (dz, dc) in enumerate(PEERS):
-            r, _ = place(dz, dc)
+    def first_turn(step, some=range(len(PEERS))):
+        for i in some:
+            r, _ = place(*PEERS[i])
 
             @pl.when(r == 0)
             def _():
@@ -229,13 +229,13 @@
         to_core.wait_recv()
         to_second.start()
 
-    first_turn(lambda copy: copy.start())
     same = [i for i, (dz, _) in enumerate(PEERS) if dz % 2 == 0]
     apart = [i for i, (dz, _) in enumerate(PEERS) if dz % 2 == 1]
     for own_lo, order in ((0, (same, apart)), (1, (apart, same))):
         @pl.when(lo == own_lo)
         def _():
             for group in order:
+                first_turn(lambda copy: copy.start(), group)
                 for turn in (1, 2):
                     for i in group:
                         cols[turn][i].start()

time: 57.4 us -> 57.4 us (level)
  no operation moved by 1% of the time
where the time goes in v7:
time: 57.4 us; the launch traced here: 57.3 us
  Pallas kernels  56.6 us (99%)
  between operations  0.64 us (1%)
    pallas_call x1, Pallas kernels, shards(): pl.pallas_call(kernel, name='whiten', out_shape=[pltpu.VMEM((width, lengt...  53.6 us
    pallas_call x1, Pallas kernels, shards(): pl.pallas_call(store, name='store', out_shape=[jax.ShapeDtypeStruct(x.sha...  3.08 us

profile of v7, /device:TPU:1, one launch (start us, length us, event | category | flops | bytes accessed | tf_op | source)
XLA Modules:
  0.0 57.3 jit_solution(15118250465296852269)
XLA Ops:
  0.6 53.6 %whiten.1 = (f32[48,8192]{1,0:T(8,128)S(1)}, f32[384,1024]{1,0:T(8,128)S(1)}, f32[2048,512]{1,0:T(8,128)S(1)}) custom-call(f32[48,8192]{1,0:T(8,128)} %bitcast.2, f32[384,1024]{1,0:T(8,128)} %s_hbm.1, f32[2048,512]{1,0:T(8,128)} %v_hbm.1), custom_call_target="tpu_custom_call" | custom-call | tf_op jit(solution)/shard_map/whiten/pallas_call | solution.py:473
  54.2 3.1 %store.1 = (f32[48,8192]{1,0:T(8,128)}, f32[384,1024]{1,0:T(8,128)}, f32[2048,512]{1,0:T(8,128)}) custom-call(f32[48,8192]{1,0:T(8,128)S(1)} %get-tuple-element.9.refs_0_, f32[384,1024]{1,0:T(8,128)S(1)} %get-tuple-element.10.refs_1_, f32[2048,512]{1,0:T(8,128)S(1)} %get-tuple-element.11.refs_2_), custom_call_target="tpu_custom_call" | custom-call | tf_op jit(solution)/shard_map/store/pallas_call | solution.py:489
